TPU v7x, 32 devices: a whole 2x2x4 slice. The times are simulated.
32 devices in a mesh: grp: 2 (over y), zt: 4 (over x, core), xy: 4 (over z).
Axes of the slice: x: 2, y: 2, z: 4, core: 2. Of those that a mesh axis runs over, the one named last changes fastest.
Arguments:
- source: float32 [2, 2, 3, 8, 16, 128], P('grp', None, None, 'xy', 'zt'), may hold values from -6 to 6
- links: float32 [4, 2, 3, 3, 8, 16, 128], P('grp', None, None, None, 'xy', 'zt'), may hold values from -2 to 2
- shifts: float32 [12], replicated, may hold values from 0.01 to 0.5
- residues: float32 [12], replicated, may hold values from 0.05 to 0.5
- mass: float32 [1], replicated, may hold values from 0.1 to 0.5
Outputs:
- rational: float32 [2, 2, 3, 8, 16, 128], P('grp', None, None, 'xy', 'zt')
- action: float32 [1], replicated
All inputs are finite; a program needn't handle non-finite values.
Results may differ from a plain program's by a relative error of at most 0.0003.
Values sent between devices are 32-bit elements; how exact they have to be, the bound alone decides.
A program may use at most 64 MiB of HBM per device.

v0:
```python
import jax
import jax.numpy as jnp
from jax import lax
from jax.sharding import PartitionSpec as P

NY = 2
NZ = 64
ITERS = 8


def shifted(block, axis, distance):
    devices = range(lax.axis_size(axis))
    route = [((i - distance) % len(devices), i) for i in devices]
    return lax.ppermute(block, axis, route)


def extended(block, sides, width):
    for axis, dim in sides:
        count = lax.axis_size(axis)
        forward = [(i, i + 1) for i in range(count - 1)]
        forward.append((count - 1, 0))
        backward = [(target, source) for source, target in forward]
        low = lax.ppermute(
            lax.slice_in_dim(block, block.shape[dim] - width, None, axis=dim), axis, forward
        )
        high = lax.ppermute(lax.slice_in_dim(block, 0, width, axis=dim), axis, backward)
        block = jnp.concatenate([low, block, high], axis=dim)
    return block


def sign_of(values):
    return (1 - 2 * (values % 2)).astype(jnp.float32)


def phases(coord_x, coord_t, last_t):
    yz_index = jnp.arange(NY * NZ, dtype=jnp.int32)
    ycoord = yz_index // NZ
    zcoord = yz_index % NZ
    unity = jnp.ones((coord_x.shape[0], coord_t.shape[0], NY * NZ), jnp.float32)
    boundary = jnp.where(coord_t == last_t, -1.0, 1.0).astype(jnp.float32)
    eta_y = sign_of(coord_x)[:, None, None] * unity
    eta_z = sign_of(coord_x[:, None, None] + ycoord[None, None, :]) * unity
    eta_t = (
        sign_of(coord_x[:, None, None] + ycoord[None, None, :] + zcoord[None, None, :])
        * boundary[None, :, None]
    )
    return jnp.stack([unity, eta_y, eta_z, eta_t])


def times_link(link, field):
    real = jnp.sum(
        link[0][None] * field[:, 0][:, None] - link[1][None] * field[:, 1][:, None], axis=2
    )
    imag = jnp.sum(
        link[0][None] * field[:, 1][:, None] + link[1][None] * field[:, 0][:, None], axis=2
    )
    return jnp.stack([real, imag], axis=1)


def times_adjoint(link, field):
    real = jnp.sum(
        link[0][None] * field[:, 0][:, :, None] + link[1][None] * field[:, 1][:, :, None], axis=1
    )
    imag = jnp.sum(
        link[0][None] * field[:, 1][:, :, None] - link[1][None] * field[:, 0][:, :, None], axis=1
    )
    return jnp.stack([real, imag], axis=1)


def roll_ycoord(values, offset):
    return jnp.roll(values, offset * NZ, axis=-1)


def roll_zcoord(values, offset):
    shape = values.shape
    return jnp.roll(values.reshape(shape[:-1] + (NY, NZ)), offset, axis=-1).reshape(shape)


def hopping(field, link):
    inner_field = field[..., 1:-1, 1:-1, :]
    inner_link = link[..., 1:-1, 1:-1, :]
    total = times_link(inner_link[0], field[..., 2:, 1:-1, :]) - times_adjoint(
        link[0][..., :-2, 1:-1, :], field[..., :-2, 1:-1, :]
    )
    total = (
        total
        + times_link(inner_link[1], roll_ycoord(inner_field, -1))
        - roll_ycoord(times_adjoint(inner_link[1], inner_field), 1)
    )
    total = (
        total
        + times_link(inner_link[2], roll_zcoord(inner_field, -1))
        - roll_zcoord(times_adjoint(inner_link[2], inner_field), 1)
    )
    total = (
        total
        + times_link(inner_link[3], field[..., 1:-1, 2:, :])
        - times_adjoint(link[3][..., 1:-1, :-2, :], field[..., 1:-1, :-2, :])
    )
    return 0.5 * total


def local_dot(left, right):
    return jnp.sum(left * right, axis=(1, 2, 3, 4, 5))


def spread(values):
    return values.reshape(values.shape + (1, 1, 1, 1, 1))


def on_device(source, links, shifts, residues, mass):
    all_links = lax.all_gather(links, "grp", axis=0, tiled=True)
    cells_x = source.shape[3]
    cells_t = source.shape[4]
    coord_x = lax.axis_index("xy") * cells_x + jnp.arange(cells_x, dtype=jnp.int32)
    coord_t = lax.axis_index("zt") * cells_t + jnp.arange(cells_t, dtype=jnp.int32)
    eta = phases(coord_x, coord_t, cells_t * lax.axis_size("zt") - 1)
    folded = all_links * eta[:, None, None, None]
    mass_sq = mass[0] * mass[0]
    rim_x = shifted(folded[0][:, :, :, -1:, :, :], "xy", 1)
    rim_t = shifted(folded[3][:, :, :, :, -1:, :], "zt", 1)
    wide_links = jnp.pad(folded, ((0, 0), (0, 0), (0, 0), (0, 0), (1, 1), (1, 1), (0, 0)))
    wide_links = wide_links.at[0, :, :, :, 0:1, 1:-1, :].set(rim_x)
    wide_links = wide_links.at[3, :, :, :, 1:-1, 0:1, :].set(rim_t)

    def with_faces(field):
        return extended(field, (("zt", 4), ("xy", 3)), 1)

    shift_col = shifts[:, None]
    members = source.shape[0]
    residual = source
    direction = source
    solutions = jnp.zeros((shifts.shape[0],) + source.shape, jnp.float32)
    directions = jnp.broadcast_to(source[None], solutions.shape)
    norm_now = lax.psum(local_dot(source, source), ("zt", "xy"))
    zeta_now = jnp.ones((shifts.shape[0], members), jnp.float32)
    zeta_old = jnp.ones((shifts.shape[0], members), jnp.float32)
    alpha_old = jnp.ones((members,), jnp.float32)
    beta_old = jnp.zeros((members,), jnp.float32)
    for iteration in range(ITERS):
        first_hop = hopping(with_faces(direction), wide_links)
        image = mass_sq * direction - hopping(with_faces(first_hop), wide_links)
        curvature_sum, cross_sum, image_sum = lax.psum(
            (local_dot(direction, image), local_dot(residual, image), local_dot(image, image)),
            ("zt", "xy"),
        )
        alpha_now = norm_now / curvature_sum
        zeta_new = (
            zeta_now
            * zeta_old
            * alpha_old
            / (
                alpha_now * beta_old * (zeta_old - zeta_now)
                + zeta_old * alpha_old * (1.0 + shift_col * alpha_now)
            )
        )
        alpha_shift = alpha_now * zeta_new / zeta_now
        solutions = solutions + spread(alpha_shift) * directions
        if iteration + 1 < ITERS:
            residual = residual - spread(alpha_now) * image
            norm_next = norm_now - 2.0 * alpha_now * cross_sum + alpha_now * alpha_now * image_sum
            beta_now = norm_next / norm_now
            beta_shift = beta_now * (zeta_new / zeta_now) ** 2
            direction = residual + spread(beta_now) * direction
            directions = spread(zeta_new) * residual[None] + spread(beta_shift) * directions
            zeta_old = zeta_now
            zeta_now = zeta_new
            alpha_old = alpha_now
            beta_old = beta_now
            norm_now = norm_next
    rational = jnp.sum(residues.reshape((-1, 1, 1, 1, 1, 1, 1)) * solutions, axis=0)
    total = lax.psum(jnp.sum(source * rational), ("grp", "zt", "xy"))
    site_count = (
        members
        * lax.axis_size("grp")
        * cells_x
        * lax.axis_size("xy")
        * cells_t
        * lax.axis_size("zt")
        * NY
        * NZ
    )
    action = (total / site_count).reshape(1)
    return (rational, action)


def solution(mesh):
    placed = (
        P("grp", None, None, "xy", "zt", None),
        P("grp", None, None, None, "xy", "zt", None),
        P(),
        P(),
        P(),
    )
    return jax.shard_map(
        on_device,
        mesh=mesh,
        in_specs=placed,
        out_specs=(P("grp", None, None, "xy", "zt", None), P()),
        check_vma=False,
    )
```

profile of v0, /device:TPU:0, one launch (start us, length us, event | category | flops | bytes accessed | tf_op | source)
XLA Modules:
  0.0 512.2 jit_solution(10780419264730769000)
XLA Ops:
  0.7 7.8 %all_gather.3 = f32[4,2,3,3,2,4,128]{6,5,4,3,2,1,0:T(4,128)S(1)} all-gather(f32[2,2,3,3,2,4,128]{6,5,4,3,2,1,0:T(4,128)} %param.10), channel_id=1, replica_groups=mesh['grp'=2,'zt'=4,'xy'=4] {'grp'}, dimensions={0}, use_global_device_ids=true | all-gather | bytes 442368 | tf_op jit(solution)/shard_map/all_gather | solution.py:112
  14.1 2.1 collective-permute-start.4
  18.0 3.9 collective-permute-done.5
  31.7 2.6 collective-permute-done.9
  36.1 30.7 %all-reduce.7 = (f32[1]{0:T(128)}, f32[1]{0:T(128)}, f32[1]{0:T(128)}) all-reduce(f32[1]{0:T(128)} %bitcast, f32[1]{0:T(128)} %bitcast.76, f32[1]{0:T(128)} %bitcast.80), channel_id=1, replica_groups=mesh['grp'=2,'zt'=4,'xy'=4] {'zt','xy'}, use_global_device_ids=true, to_apply=%region_1.2 | all-reduce | flops 3 | bytes 24 | tf_op jit(solution)/shard_map/psum | solution.py:135
  78.4 3.0 collective-permute-done.13
  89.1 2.0 collective-permute-done.16
  91.1 2.3 collective-permute-done.17
  95.2 30.6 %all-reduce.6 = (f32[1]{0:T(128)}, f32[1]{0:T(128)}, f32[1]{0:T(128)}) all-reduce(f32[1]{0:T(128)} %bitcast.140, f32[1]{0:T(128)} %bitcast.144, f32[1]{0:T(128)} %bitcast.145), channel_id=1, replica_groups=mesh['grp'=2,'zt'=4,'xy'=4] {'zt','xy'}, use_global_device_ids=true, to_apply=%region_71.72 | all-reduce | flops 3 | bytes 24 | tf_op jit(solution)/shard_map/psum | solution.py:143
  135.4 2.8 collective-permute-done.21
  147.7 2.5 collective-permute-done.25
  152.0 30.4 %all-reduce.5 = (f32[1]{0:T(128)}, f32[1]{0:T(128)}, f32[1]{0:T(128)}) all-reduce(f32[1]{0:T(128)} %bitcast.205, f32[1]{0:T(128)} %bitcast.209, f32[1]{0:T(128)} %bitcast.210), channel_id=1, replica_groups=mesh['grp'=2,'zt'=4,'xy'=4] {'zt','xy'}, use_global_device_ids=true, to_apply=%region_109.110 | all-reduce | flops 3 | bytes 24 | tf_op jit(solution)/shard_map/psum | solution.py:143
  192.2 3.1 collective-permute-done.29
  203.0 2.0 collective-permute-done.32
  205.0 2.3 collective-permute-done.33
  209.2 30.6 %all-reduce.4 = (f32[1]{0:T(128)}, f32[1]{0:T(128)}, f32[1]{0:T(128)}) all-reduce(f32[1]{0:T(128)} %bitcast.270, f32[1]{0:T(128)} %bitcast.274, f32[1]{0:T(128)} %bitcast.275), channel_id=1, replica_groups=mesh['grp'=2,'zt'=4,'xy'=4] {'zt','xy'}, use_global_device_ids=true, to_apply=%region_147.148 | all-reduce | flops 3 | bytes 24 | tf_op jit(solution)/shard_map/psum | solution.py:143
  249.3 2.8 collective-permute-done.37
  261.7 2.5 collective-permute-done.41
  265.9 30.4 %all-reduce.3 = (f32[1]{0:T(128)}, f32[1]{0:T(128)}, f32[1]{0:T(128)}) all-reduce(f32[1]{0:T(128)} %bitcast.335, f32[1]{0:T(128)} %bitcast.339, f32[1]{0:T(128)} %bitcast.340), channel_id=1, replica_groups=mesh['grp'=2,'zt'=4,'xy'=4] {'zt','xy'}, use_global_device_ids=true, to_apply=%region_185.186 | all-reduce | flops 3 | bytes 24 | tf_op jit(solution)/shard_map/psum | solution.py:143
  306.2 3.1 collective-permute-done.45
  317.0 2.0 collective-permute-done.48
  319.0 2.3 collective-permute-done.49
  323.1 30.6 %all-reduce.2 = (f32[1]{0:T(128)}, f32[1]{0:T(128)}, f32[1]{0:T(128)}) all-reduce(f32[1]{0:T(128)} %bitcast.400, f32[1]{0:T(128)} %bitcast.404, f32[1]{0:T(128)} %bitcast.405), channel_id=1, replica_groups=mesh['grp'=2,'zt'=4,'xy'=4] {'zt','xy'}, use_global_device_ids=true, to_apply=%region_223.224 | all-reduce | flops 3 | bytes 24 | tf_op jit(solution)/shard_map/psum | solution.py:143
  363.4 2.8 collective-permute-done.53
  373.9 1.8 collective-permute-done.56
  375.7 2.5 collective-permute-done.57
  380.0 30.4 %all-reduce.1 = (f32[1]{0:T(128)}, f32[1]{0:T(128)}, f32[1]{0:T(128)}) all-reduce(f32[1]{0:T(128)} %bitcast.465, f32[1]{0:T(128)} %bitcast.469, f32[1]{0:T(128)} %bitcast.470), channel_id=1, replica_groups=mesh['grp'=2,'zt'=4,'xy'=4] {'zt','xy'}, use_global_device_ids=true, to_apply=%region_261.262 | all-reduce | flops 3 | bytes 24 | tf_op jit(solution)/shard_map/psum | solution.py:143
  420.2 3.1 collective-permute-done.61
  430.9 2.0 collective-permute-done.64
  432.9 2.3 collective-permute-done.65
  437.0 30.6 %psum.185 = f32[1]{0:T(128)} all-reduce(f32[1]{0:T(128)} %bitcast.531), channel_id=1, replica_groups=mesh['grp'=2,'zt'=4,'xy'=4] {'zt','xy'}, use_global_device_ids=true, to_apply=%region_299.300 | all-reduce | flops 1 | bytes 8 | tf_op jit(solution)/shard_map/psum | solution.py:143
  469.9 40.5 %psum.186 = f32[]{:T(128)} all-reduce(f32[]{:T(128)} %multiply_reduce_fusion.1), channel_id=1, replica_groups=mesh['grp'=2,'zt'=4,'xy'=4] {'grp','zt','xy'}, use_global_device_ids=true, to_apply=%region_302.303 | all-reduce | flops 1 | bytes 8 | tf_op jit(solution)/shard_map/psum | solution.py:172
  (731 shorter events, 141.5 us)
Async XLA Ops:
  8.8 13.1 %collective-permute-start = (f32[2,3,3,1,4,128]{5,4,3,2,1,0:T(4,128)S(1)}, f32[2,3,3,1,4,128]{5,4,3,2,1,0:T(4,128)S(1)}, u32[]{:S(2)}, u32[]{:S(2)}) collective-permute-start(f32[2,3,3,1,4,128]{5,4,3,2,1,0:T(4,128)S(1)} %slice.3115), channel_id=1, source_target_pairs={{3,0},{0,1},{1,2},{2,3},{7,4},{4,5},{5,6},{6,7},{11,8},{8,9},{9,10... | collective-permute-start | bytes 110600 | tf_op jit(solution)/shard_map/ppermute | solution.py:14
  10.7 11.4 %collective-permute-start.1 = (f32[2,3,3,2,1,128]{5,4,3,2,1,0:T(1,128)S(1)}, f32[2,3,3,2,1,128]{5,4,3,2,1,0:T(1,128)S(1)}, u32[]{:S(2)}, u32[]{:S(2)}) collective-permute-start(f32[2,3,3,2,1,128]{5,4,3,2,1,0:T(1,128)S(1)} %slice.3117), channel_id=1, source_target_pairs={{12,0},{0,4},{4,8},{8,12},{13,1},{1,5},{5,9},{9,13},{14,2},{2,6},{... | collective-permute-start | bytes 55304 | tf_op jit(solution)/shard_map/ppermute | solution.py:14
  14.1 3.9 collective-permute-start.4
  16.2 5.6 %collective-permute-start.5 = (f32[1,2,3,1,6,128]{5,4,3,2,1,0:T(8,128)S(1)}, f32[1,2,3,1,6,128]{5,4,3,2,1,0:T(8,128)S(1)}, u32[]{:S(2)}, u32[]{:S(2)}) collective-permute-start(f32[1,2,3,1,6,128]{5,4,3,2,1,0:T(8,128)S(1)} %get-tuple-element.617), channel_id=1, source_target_pairs={{0,1},{1,2},{2,3},{3,0},{4,5},{5,6},{6,7},{7,4},{8,9},{9,10},{10,1... | collective-permute-start | bytes 55304 | tf_op jit(solution)/shard_map/ppermute | solution.py:23
  27.9 3.9 collective-permute-start.8
  28.6 5.8 %collective-permute-start.9 = (f32[1,2,3,1,6,128]{5,4,3,2,1,0:T(8,128)S(1)}, f32[1,2,3,1,6,128]{5,4,3,2,1,0:T(8,128)S(1)}, u32[]{:S(2)}, u32[]{:S(2)}) collective-permute-start(f32[1,2,3,1,6,128]{5,4,3,2,1,0:T(8,128)S(1)} %get-tuple-element.613), channel_id=1, source_target_pairs={{0,1},{1,2},{2,3},{3,0},{4,5},{5,6},{6,7},{7,4},{8,9},{9,10},{10,1... | collective-permute-start | bytes 55304 | tf_op jit(solution)/shard_map/ppermute | solution.py:23
  74.5 3.9 collective-permute-start.12
  75.5 5.8 %collective-permute-start.13 = (f32[1,2,3,1,6,128]{5,4,3,2,1,0:T(8,128)S(1)}, f32[1,2,3,1,6,128]{5,4,3,2,1,0:T(8,128)S(1)}, u32[]{:S(2)}, u32[]{:S(2)}) collective-permute-start(f32[1,2,3,1,6,128]{5,4,3,2,1,0:T(8,128)S(1)} %get-tuple-element.609), channel_id=1, source_target_pairs={{0,1},{1,2},{2,3},{3,0},{4,5},{5,6},{6,7},{7,4},{8,9},{9,10},{10,1... | collective-permute-start | bytes 55304 | tf_op jit(solution)/shard_map/ppermute | solution.py:23
  87.0 4.1 collective-permute-start.16
  87.6 5.8 %collective-permute-start.17 = (f32[1,2,3,1,6,128]{5,4,3,2,1,0:T(8,128)S(1)}, f32[1,2,3,1,6,128]{5,4,3,2,1,0:T(8,128)S(1)}, u32[]{:S(2)}, u32[]{:S(2)}) collective-permute-start(f32[1,2,3,1,6,128]{5,4,3,2,1,0:T(8,128)S(1)} %get-tuple-element.605), channel_id=1, source_target_pairs={{0,1},{1,2},{2,3},{3,0},{4,5},{5,6},{6,7},{7,4},{8,9},{9,10},{10,1... | collective-permute-start | bytes 55304 | tf_op jit(solution)/shard_map/ppermute | solution.py:23
  131.5 3.9 collective-permute-start.20
  132.5 5.6 %collective-permute-start.21 = (f32[1,2,3,1,6,128]{5,4,3,2,1,0:T(8,128)S(1)}, f32[1,2,3,1,6,128]{5,4,3,2,1,0:T(8,128)S(1)}, u32[]{:S(2)}, u32[]{:S(2)}) collective-permute-start(f32[1,2,3,1,6,128]{5,4,3,2,1,0:T(8,128)S(1)} %get-tuple-element.601), channel_id=1, source_target_pairs={{0,1},{1,2},{2,3},{3,0},{4,5},{5,6},{6,7},{7,4},{8,9},{9,10},{10,1... | collective-permute-start | bytes 55304 | tf_op jit(solution)/shard_map/ppermute | solution.py:23
  143.8 3.9 collective-permute-start.24
  144.6 5.6 %collective-permute-start.25 = (f32[1,2,3,1,6,128]{5,4,3,2,1,0:T(8,128)S(1)}, f32[1,2,3,1,6,128]{5,4,3,2,1,0:T(8,128)S(1)}, u32[]{:S(2)}, u32[]{:S(2)}) collective-permute-start(f32[1,2,3,1,6,128]{5,4,3,2,1,0:T(8,128)S(1)} %get-tuple-element.597), channel_id=1, source_target_pairs={{0,1},{1,2},{2,3},{3,0},{4,5},{5,6},{6,7},{7,4},{8,9},{9,10},{10,1... | collective-permute-start | bytes 55304 | tf_op jit(solution)/shard_map/ppermute | solution.py:23
  188.2 4.1 collective-permute-start.28
  189.4 5.8 %collective-permute-start.29 = (f32[1,2,3,1,6,128]{5,4,3,2,1,0:T(8,128)S(1)}, f32[1,2,3,1,6,128]{5,4,3,2,1,0:T(8,128)S(1)}, u32[]{:S(2)}, u32[]{:S(2)}) collective-permute-start(f32[1,2,3,1,6,128]{5,4,3,2,1,0:T(8,128)S(1)} %get-tuple-element.593), channel_id=1, source_target_pairs={{0,1},{1,2},{2,3},{3,0},{4,5},{5,6},{6,7},{7,4},{8,9},{9,10},{10,1... | collective-permute-start | bytes 55304 | tf_op jit(solution)/shard_map/ppermute | solution.py:23
  200.9 4.1 collective-permute-start.32
  201.5 5.9 %collective-permute-start.33 = (f32[1,2,3,1,6,128]{5,4,3,2,1,0:T(8,128)S(1)}, f32[1,2,3,1,6,128]{5,4,3,2,1,0:T(8,128)S(1)}, u32[]{:S(2)}, u32[]{:S(2)}) collective-permute-start(f32[1,2,3,1,6,128]{5,4,3,2,1,0:T(8,128)S(1)} %get-tuple-element.589), channel_id=1, source_target_pairs={{0,1},{1,2},{2,3},{3,0},{4,5},{5,6},{6,7},{7,4},{8,9},{9,10},{10,1... | collective-permute-start | bytes 55304 | tf_op jit(solution)/shard_map/ppermute | solution.py:23
  246.5 5.6 %collective-permute-start.37 = (f32[1,2,3,1,6,128]{5,4,3,2,1,0:T(8,128)S(1)}, f32[1,2,3,1,6,128]{5,4,3,2,1,0:T(8,128)S(1)}, u32[]{:S(2)}, u32[]{:S(2)}) collective-permute-start(f32[1,2,3,1,6,128]{5,4,3,2,1,0:T(8,128)S(1)} %get-tuple-element.585), channel_id=1, source_target_pairs={{0,1},{1,2},{2,3},{3,0},{4,5},{5,6},{6,7},{7,4},{8,9},{9,10},{10,1... | collective-permute-start | bytes 55304 | tf_op jit(solution)/shard_map/ppermute | solution.py:23
  257.8 3.9 collective-permute-start.40
  258.6 5.6 %collective-permute-start.41 = (f32[1,2,3,1,6,128]{5,4,3,2,1,0:T(8,128)S(1)}, f32[1,2,3,1,6,128]{5,4,3,2,1,0:T(8,128)S(1)}, u32[]{:S(2)}, u32[]{:S(2)}) collective-permute-start(f32[1,2,3,1,6,128]{5,4,3,2,1,0:T(8,128)S(1)} %get-tuple-element.581), channel_id=1, source_target_pairs={{0,1},{1,2},{2,3},{3,0},{4,5},{5,6},{6,7},{7,4},{8,9},{9,10},{10,1... | collective-permute-start | bytes 55304 | tf_op jit(solution)/shard_map/ppermute | solution.py:23
  302.1 4.1 collective-permute-start.44
  303.4 5.9 %collective-permute-start.45 = (f32[1,2,3,1,6,128]{5,4,3,2,1,0:T(8,128)S(1)}, f32[1,2,3,1,6,128]{5,4,3,2,1,0:T(8,128)S(1)}, u32[]{:S(2)}, u32[]{:S(2)}) collective-permute-start(f32[1,2,3,1,6,128]{5,4,3,2,1,0:T(8,128)S(1)} %get-tuple-element.577), channel_id=1, source_target_pairs={{0,1},{1,2},{2,3},{3,0},{4,5},{5,6},{6,7},{7,4},{8,9},{9,10},{10,1... | collective-permute-start | bytes 55304 | tf_op jit(solution)/shard_map/ppermute | solution.py:23
  314.9 4.1 collective-permute-start.48
  315.5 5.9 %collective-permute-start.49 = (f32[1,2,3,1,6,128]{5,4,3,2,1,0:T(8,128)S(1)}, f32[1,2,3,1,6,128]{5,4,3,2,1,0:T(8,128)S(1)}, u32[]{:S(2)}, u32[]{:S(2)}) collective-permute-start(f32[1,2,3,1,6,128]{5,4,3,2,1,0:T(8,128)S(1)} %get-tuple-element.573), channel_id=1, source_target_pairs={{0,1},{1,2},{2,3},{3,0},{4,5},{5,6},{6,7},{7,4},{8,9},{9,10},{10,1... | collective-permute-start | bytes 55304 | tf_op jit(solution)/shard_map/ppermute | solution.py:23
  360.6 5.6 %collective-permute-start.53 = (f32[1,2,3,1,6,128]{5,4,3,2,1,0:T(8,128)S(1)}, f32[1,2,3,1,6,128]{5,4,3,2,1,0:T(8,128)S(1)}, u32[]{:S(2)}, u32[]{:S(2)}) collective-permute-start(f32[1,2,3,1,6,128]{5,4,3,2,1,0:T(8,128)S(1)} %get-tuple-element.569), channel_id=1, source_target_pairs={{0,1},{1,2},{2,3},{3,0},{4,5},{5,6},{6,7},{7,4},{8,9},{9,10},{10,1... | collective-permute-start | bytes 55304 | tf_op jit(solution)/shard_map/ppermute | solution.py:23
  371.8 3.9 collective-permute-start.56
  372.7 5.6 %collective-permute-start.57 = (f32[1,2,3,1,6,128]{5,4,3,2,1,0:T(8,128)S(1)}, f32[1,2,3,1,6,128]{5,4,3,2,1,0:T(8,128)S(1)}, u32[]{:S(2)}, u32[]{:S(2)}) collective-permute-start(f32[1,2,3,1,6,128]{5,4,3,2,1,0:T(8,128)S(1)} %get-tuple-element.565), channel_id=1, source_target_pairs={{0,1},{1,2},{2,3},{3,0},{4,5},{5,6},{6,7},{7,4},{8,9},{9,10},{10,1... | collective-permute-start | bytes 55304 | tf_op jit(solution)/shard_map/ppermute | solution.py:23
  416.2 4.0 collective-permute-start.60
  417.4 5.9 %collective-permute-start.61 = (f32[1,2,3,1,6,128]{5,4,3,2,1,0:T(8,128)S(1)}, f32[1,2,3,1,6,128]{5,4,3,2,1,0:T(8,128)S(1)}, u32[]{:S(2)}, u32[]{:S(2)}) collective-permute-start(f32[1,2,3,1,6,128]{5,4,3,2,1,0:T(8,128)S(1)} %get-tuple-element.559), channel_id=1, source_target_pairs={{0,1},{1,2},{2,3},{3,0},{4,5},{5,6},{6,7},{7,4},{8,9},{9,10},{10,1... | collective-permute-start | bytes 55304 | tf_op jit(solution)/shard_map/ppermute | solution.py:23
  428.8 4.1 collective-permute-start.64
  429.4 5.9 %collective-permute-start.65 = (f32[1,2,3,1,6,128]{5,4,3,2,1,0:T(8,128)S(1)}, f32[1,2,3,1,6,128]{5,4,3,2,1,0:T(8,128)S(1)}, u32[]{:S(2)}, u32[]{:S(2)}) collective-permute-start(f32[1,2,3,1,6,128]{5,4,3,2,1,0:T(8,128)S(1)} %get-tuple-element.555), channel_id=1, source_target_pairs={{0,1},{1,2},{2,3},{3,0},{4,5},{5,6},{6,7},{7,4},{8,9},{9,10},{10,1... | collective-permute-start | bytes 55304 | tf_op jit(solution)/shard_map/ppermute | solution.py:23
  (38 other events, 233.6 us)
where the time goes:
time: 513 us; the launch traced here: 512 us
  blocking collectives  293 us (57%)
  waiting for transfers between devices  89.2 us (17%)
  starting transfers between devices  64.4 us (13%)
  local copies, waits for them, and re-layouts  22.3 us (4%)
  between operations  22 us (4%)
  other arithmetic  21.7 us (4%)
    psum x7, blocking collectives, on_device(): lax.psum((local_dot(direction, image), local_dot(residual, image), local_...  214 us
    ppermute x32, waiting for transfers between devices, extended(): lax.ppermute(lax.slice_in_dim(block, block.shape[dim] - width, None, axis...  59.6 us
    ppermute x32, starting transfers between devices, extended(): lax.ppermute(lax.slice_in_dim(block, 0, width, axis=dim), axis, backward)  41.5 us
    psum x1, blocking collectives, on_device(): total = lax.psum(jnp.sum(source * rational), ('grp', 'zt', 'xy'))  40.5 us
    psum x1, blocking collectives, on_device(): norm_now = lax.psum(local_dot(source, source), ('zt', 'xy'))  30.7 us
    ppermute x32, waiting for transfers between devices, extended(): lax.ppermute(lax.slice_in_dim(block, 0, width, axis=dim), axis, backward)  29.6 us
    ppermute x32, starting transfers between devices, extended(): lax.ppermute(lax.slice_in_dim(block, block.shape[dim] - width, None, axis...  21 us
  transfers between devices with their start and end apart: 66, of which 47 were waited for; matrix products, arithmetic and copies ran while one was open for 1% of the time, Pallas kernels for 0%

commit v1 on v0

v1 whole, which is shorter than its diff:
```python
import functools

import jax
import jax.numpy as jnp
from jax import lax
from jax.experimental import pallas as pl
from jax.experimental.pallas import tpu as pltpu
from jax.sharding import PartitionSpec as P

NY = 2
NZ = 64
ITERS = 8
PAIRS = 9
MAT = 2 * PAIRS
COMPS = 6


def roll(value, shift, axis):
    size = value.shape[axis]
    return pltpu.roll(value, shift % size, axis)


def kernel(
    dims, source_ref, links_ref, shifts_ref, residues_ref, mass_ref, out_ref, action_ref,
    lk, tfar, xfar, xtwo, sx, sx2, cs_ll, cs_hl, cs_lh, c_ll, c_hl, c_lh,
    gauge, dirn, resid, mid, shiftdirs, rpack, ws, wr, cs, cr, part, act,
    state, lsend, lrecv, hsend, hrecv, psend, precv, asend, arecv,
):
    n_grp, n_zt, n_xy, cells_x, cells_t = dims
    lanes = NY * NZ
    n_all = n_zt * n_xy
    nshift = shifts_ref.shape[0]
    g = lax.axis_index("grp")
    zt = lax.axis_index("zt")
    xy = lax.axis_index("xy")
    me = zt * n_xy + xy
    me_all = g * n_all + me
    x_up, x_dn = lax.rem(xy + 1, n_xy), lax.rem(xy + n_xy - 1, n_xy)
    t_up, t_dn = lax.rem(zt + 1, n_zt), lax.rem(zt + n_zt - 1, n_zt)
    other = 1 - g

    def place(linear):
        inside = lax.rem(linear, n_all)
        return (linear // n_all, inside // n_xy, lax.rem(inside, n_xy))

    def each(count, fn):
        if count <= 32:
            for p in range(1, count):
                fn(p)
        else:
            def step(p, carry):
                fn(p)
                return carry
            lax.fori_loop(1, count, step, 0)

    def copy(src, dst, send, recv, device):
        return pltpu.make_async_remote_copy(
            src_ref=src, dst_ref=dst, send_sem=send, recv_sem=recv,
            device_id=device, device_id_type=pl.DeviceIdType.MESH,
        )

    barrier = pltpu.get_barrier_semaphore()

    def greet(p):
        pl.semaphore_signal(
            barrier, inc=1, device_id=place(lax.rem(me_all + p, n_grp * n_all)),
            device_id_type=pl.DeviceIdType.MESH,
        )

    each(n_grp * n_all, greet)

    sub = lax.broadcasted_iota(jnp.int32, (8, lanes), 0)
    lane = lax.broadcasted_iota(jnp.int32, (8, lanes), 1)
    zcoord = lax.rem(lane, NZ)
    ycoord = lane // NZ
    own = (sub >= 2) & (sub < 2 + cells_t)
    first = sub < cells_t
    late = lax.rem(sub, cells_t) >= 2

    for d in range(2):
        for c in range(MAT):
            low, high = links_ref[c], links_ref[MAT + c]
            if d == 0:
                sx[0, pl.ds(g * MAT + c, 1)] = jnp.where(first, roll(low, 4, 0), high)[None]
            else:
                sx[1, pl.ds(g * MAT + c, 1)] = jnp.where(first, low, roll(high, 4, 0))[None]
    for c in range(2 * MAT):
        lk[pl.ds(g * 2 * MAT + c, 1)] = links_ref[c][None]

    spack = [source_ref[c] for c in range(COMPS)]

    def corner_tiles(tiles, par):
        for k, row in enumerate((7, 4, 3, 0)):
            tile = jnp.zeros((8, lanes), jnp.float32)
            for c in range(COMPS):
                tile = jnp.where(sub == c, jnp.broadcast_to(tiles[c][row:row + 1], (8, lanes)), tile)
            cs[par, k] = tile

    corner_dev = ((g, t_up, x_up), (g, t_dn, x_up), (g, t_up, x_dn), (g, t_dn, x_dn))

    def halo(par):
        routes = ((g, zt, x_up), (g, zt, x_dn), (g, t_up, xy), (g, t_dn, xy))
        found = []
        for k in range(4):
            found.append(copy(cs.at[par, k], cr.at[par, k], hsend.at[par, 4 + k], hrecv.at[par, 4 + k], corner_dev[k]))
        for k in range(4):
            found.append(copy(ws.at[par], wr.at[par, k], hsend.at[par, k], hrecv.at[par, k], routes[k]))
        return found

    def send_part(par):
        def go(p):
            copy(part.at[par, me], part.at[par, me], psend.at[par, p], precv.at[par, me],
                 (g,) + place(lax.rem(me + p, n_all))[1:]).start()
        each(n_all, go)

    def wait_part(par):
        def go(p):
            there = lax.rem(me + n_all - p, n_all)
            done = copy(part.at[par, there], part.at[par, there], psend.at[par, p], precv.at[par, there],
                        (g,) + place(there)[1:])
            done.wait_recv()
            done.wait_send()
        each(n_all, go)

    def dots(rows):
        tile = jnp.zeros((8, lanes), jnp.float32)
        for k, row in enumerate(rows):
            tile = jnp.where(sub == k, jnp.broadcast_to(jnp.sum(row, axis=0, keepdims=True), (8, lanes)), tile)
        return tile

    def summed(ref, par, count):
        if count <= 32:
            total = ref[par, 0]
            for j in range(1, count):
                total = total + ref[par, j]
        else:
            total = lax.fori_loop(1, count, lambda j, acc: acc + ref[par, j], ref[par, 0])
        return jnp.broadcast_to(jnp.sum(total, axis=1, keepdims=True), (8, lanes))

    def fill(values, k):
        return jnp.broadcast_to(values[k:k + 1], (16, lanes))

    def inner(left, right):
        total = left[0] * right[0]
        for c in range(1, COMPS):
            total = total + left[c] * right[c]
        return total

    corner_tiles(spack, 0)
    for c in range(COMPS):
        ws[0, c] = spack[c]
    part[0, pl.ds(me, 1)] = dots([inner(spack, spack)])[None]

    pl.semaphore_wait(barrier, n_grp * n_all - 1)

    half = 2 * MAT
    to_pair = copy(links_ref, lk.at[pl.ds(g * half, half)], lsend.at[0], lrecv.at[0], (other, zt, xy))
    to_pair.start()

    def link_faces(h, src, slot):
        return [
            copy(sx.at[0, pl.ds(h * MAT, MAT)], xfar.at[0, pl.ds(h * MAT, MAT)], lsend.at[slot], lrecv.at[slot], (g, zt, x_up)),
            copy(sx.at[1, pl.ds(h * MAT, MAT)], xfar.at[1, pl.ds(h * MAT, MAT)], lsend.at[slot + 1], lrecv.at[slot + 1], (g, zt, x_dn)),
            copy(src, tfar.at[0, pl.ds(h * half, half)], lsend.at[slot + 2], lrecv.at[slot + 2], (g, t_up, xy)),
            copy(src, tfar.at[1, pl.ds(h * half, half)], lsend.at[slot + 3], lrecv.at[slot + 3], (g, t_dn, xy)),
        ]

    near = link_faces(g, links_ref, 1)
    for item in near:
        item.start()
    send_part(0)
    for item in halo(0):
        item.start()

    to_pair.wait_recv()
    for c in range(MAT):
        low, high = lk[other * half + c], lk[other * half + MAT + c]
        sx[0, pl.ds(other * MAT + c, 1)] = jnp.where(first, roll(low, 4, 0), high)[None]
        sx[1, pl.ds(other * MAT + c, 1)] = jnp.where(first, low, roll(high, 4, 0))[None]
    for c in range(PAIRS):
        sx2[c] = jnp.where(first, lk[c], roll(lk[PAIRS + c], 4, 0))
    for c in range(MAT):
        cs_ll[c:c + 1] = lk[c][7:8]
        cs_ll[MAT + c:MAT + c + 1] = lk[3 * MAT + c][7:8]
        cs_hl[c:c + 1] = lk[3 * MAT + c][3:4]
        cs_lh[c:c + 1] = lk[c][4:5]
    far = link_faces(other, lk.at[pl.ds(other * half, half)], 5) + [
        copy(sx2, xtwo, lsend.at[9], lrecv.at[9], (g, zt, x_up)),
        copy(cs_ll, c_ll, lsend.at[10], lrecv.at[10], corner_dev[0]),
        copy(cs_hl, c_hl, lsend.at[11], lrecv.at[11], corner_dev[2]),
        copy(cs_lh, c_lh, lsend.at[12], lrecv.at[12], corner_dev[1]),
    ]
    for item in far:
        item.start()

    def pick(ref, c):
        return jnp.broadcast_to(ref[c:c + 1], (8, lanes))

    def widen(c, x, mine, low, high):
        between = jnp.where(late, low, high)
        return jnp.where(own, roll(mine, 2 - 4 * x, 0), roll(between, 6 - 4 * x, 0))

    def far_rows(block, low_corner, high_corner, x):
        row = jnp.where(own, roll(block, 2 - 4 * x, 0), 0.0)
        if low_corner is not None:
            row = jnp.where(sub == 1, low_corner, row)
        if high_corner is not None:
            row = jnp.where(sub == 6, high_corner, row)
        return row

    def extend(par, c):
        mine = ws[par, c]
        corner = [jnp.broadcast_to(cr[par, k, c:c + 1], (8, lanes)) for k in range(4)]
        return [
            far_rows(wr[par, 0, c], None, None, 0),
            far_rows(wr[par, 0, c], corner[0], corner[1], 1),
            widen(c, 0, mine, wr[par, 2, c], wr[par, 3, c]),
            widen(c, 1, mine, wr[par, 2, c], wr[par, 3, c]),
            far_rows(wr[par, 1, c], corner[2], corner[3], 0),
            far_rows(wr[par, 1, c], None, None, 1),
        ]

    rows16 = lax.broadcasted_iota(jnp.int32, (16, lanes), 0)
    shift_rows = jnp.zeros((16, lanes), jnp.float32)
    residue_rows = jnp.zeros((16, lanes), jnp.float32)
    for k in range(nshift):
        shift_rows = jnp.where(rows16 == k, shifts_ref[k], shift_rows)
        residue_rows = jnp.where(rows16 == k, residues_ref[k], residue_rows)
    mass_sq = mass_ref[0] * mass_ref[0]

    for c in range(COMPS):
        rpack[c] = spack[c]
        out_ref[c] = jnp.zeros((8, lanes), jnp.float32)
        for k in range(nshift):
            shiftdirs[k, c] = spack[c]

    for item in near + far:
        item.wait()
    to_pair.wait_send()

    t_at = lax.rem(zt * cells_t + sub - 2 + n_zt * cells_t, n_zt * cells_t)
    edge = jnp.where(t_at == n_zt * cells_t - 1, -0.5, 0.5)
    yz_sign = (1 - 2 * lax.rem(ycoord + zcoord, 2)).astype(jnp.float32)
    y_sign = (1 - 2 * lax.rem(ycoord, 2)).astype(jnp.float32)

    def z_up(v):
        cond = jnp.broadcast_to(zcoord == NZ - 1, v.shape)
        return jnp.where(cond, roll(v, NZ - 1, v.ndim - 1), roll(v, -1, v.ndim - 1))

    def z_dn(v):
        cond = jnp.broadcast_to(zcoord == 0, v.shape)
        return jnp.where(cond, roll(v, 1 - NZ, v.ndim - 1), roll(v, 1, v.ndim - 1))

    def wide_link(d, c, e):
        at = d * MAT + c
        sign = -1.0 if e % 2 else 1.0
        if e in (2, 3):
            value = widen(c, e - 2, lk[at], tfar[0, at], tfar[1, at])
        elif e == 0:
            value = far_rows(xtwo[c % PAIRS], None, None, c // PAIRS)
        elif e == 1:
            low = pick(c_ll, c) if d == 0 else (pick(c_ll, MAT + c) if d == 3 else None)
            value = far_rows(xfar[0, (d // 2) * MAT + c], low, pick(c_lh, c) if d == 0 else None, d % 2)
        else:
            value = far_rows(xfar[1, (d // 2) * MAT + c], pick(c_hl, c) if d == 3 else None, None, d % 2)
        if d == 0:
            return 0.5 * value
        if d == 1:
            return (0.5 * sign) * value
        if d == 2:
            return (0.5 * sign) * y_sign * value
        return sign * yz_sign * edge * value

    for part_no in range(2):
        for i in range(3):
            for j in range(3):
                c = part_no * PAIRS + i * 3 + j
                flip = part_no * PAIRS + j * 3 + i
                back = 1.0 if part_no else -1.0
                for e in range(0, 5):
                    wx = wide_link(0, c, e)
                    if e > 0:
                        gauge[0, c, e - 1] = wx
                    if e < 4:
                        gauge[1, flip, e] = back * wx
                for e in range(1, 5):
                    wz = wide_link(2, c, e)
                    gauge[3, c, e - 1] = wz
                    gauge[4, flip, e - 1] = back * z_dn(wz)
                    wt = wide_link(3, c, e)
                    gauge[5, c, e - 1] = wt
                    gauge[6, flip, e - 1] = back * roll(wt, 1, 0)
                    wy = wide_link(1, c, e)
                    turned = wide_link(1, flip, e)
                    gauge[2, c, e - 1] = wy + back * roll(turned, NZ, 1)

    def finish_halo(par):
        for item in halo(par):
            item.wait()

    wait_part(0)
    finish_halo(0)
    for c in range(COMPS):
        wide = extend(0, c)
        for e in range(6):
            dirn[c, e] = wide[e]
            resid[c, e] = wide[e]
    norm = fill(summed(part, 0, n_all), 0)

    def hop(field, e0):
        total = [None] * COMPS
        terms = (
            (0, lambda c: field[c, e0 + 1:e0 + 3]),
            (1, lambda c: field[c, e0 - 1:e0 + 1]),
            (2, lambda c: roll(field[c, e0:e0 + 2], NZ, 2)),
            (3, lambda c: z_up(field[c, e0:e0 + 2])),
            (4, lambda c: z_dn(field[c, e0:e0 + 2])),
            (5, lambda c: roll(field[c, e0:e0 + 2], -1, 1)),
            (6, lambda c: roll(field[c, e0:e0 + 2], 1, 1)),
        )
        for term, shifted in terms:
            v = [shifted(c) for c in range(COMPS)]
            for i in range(3):
                for j in range(3):
                    wre = gauge[term, i * 3 + j, e0 - 1:e0 + 1]
                    wim = gauge[term, PAIRS + i * 3 + j, e0 - 1:e0 + 1]
                    re = wre * v[j] - wim * v[3 + j]
                    im = wre * v[3 + j] + wim * v[j]
                    total[i] = re if total[i] is None else total[i] + re
                    total[3 + i] = im if total[3 + i] is None else total[3 + i] + im
        return total

    def image_of():
        for e0 in (1, 3):
            for c, value in enumerate(hop(dirn, e0)):
                mid[c, e0:e0 + 2] = value
        image = hop(mid, 2)
        packed = []
        dpack = []
        for c in range(COMPS):
            d2, d3 = dirn[c, 2], dirn[c, 3]
            dp = jnp.where(first, roll(d2, -2, 0), roll(d3, 2, 0))
            wp = jnp.where(first, roll(image[c][0], -2, 0), roll(image[c][1], 2, 0))
            dpack.append(dp)
            packed.append(mass_sq * dp - wp)
        return packed, dpack

    def row(values, k):
        return jnp.broadcast_to(values[k:k + 1], (8, lanes))

    def accumulate(gain):
        for c in range(COMPS):
            total = out_ref[c]
            for k in range(nshift):
                total = total + row(gain, k) * shiftdirs[k, c]
            out_ref[c] = total

    def catch_up(gain, zeta_now, beta_shift):
        accumulate(gain)
        for k in range(nshift):
            zk, bk = row(zeta_now, k), row(beta_shift, k)
            for c in range(COMPS):
                shiftdirs[k, c] = zk * rpack[c] + bk * shiftdirs[k, c]

    def iterate(step, last):
        norm, zeta, zeta_old, alpha_old, beta_old, gain, beta_shift = [state[k] for k in range(7)]
        par = step % 2 if last else lax.rem(step, 2)
        packed, dpack = image_of()
        res = [rpack[c] for c in range(COMPS)]
        part[par, pl.ds(me, 1)] = dots([inner(dpack, packed), inner(res, packed), inner(packed, packed)])[None]
        send_part(par)
        if not last:
            corner_tiles(packed, par)
            for c in range(COMPS):
                ws[par, c] = packed[c]
            for item in halo(par):
                item.start()
        catch_up(gain, zeta, beta_shift)
        wait_part(par)
        sums = summed(part, par, n_all)
        alpha = norm / fill(sums, 0)
        zeta_new = zeta * zeta_old * alpha_old / (
            alpha * beta_old * (zeta_old - zeta) + zeta_old * alpha_old * (1.0 + shift_rows * alpha)
        )
        ratio = zeta_new / zeta
        gain = residue_rows * alpha * ratio
        if last:
            return gain
        norm_next = norm - 2.0 * alpha * fill(sums, 1) + alpha * alpha * fill(sums, 2)
        beta = norm_next / norm
        beta_shift = beta * ratio * ratio
        finish_halo(par)
        step_a, step_b = row(alpha, 0), row(beta, 0)
        for c in range(COMPS):
            rpack[c] = rpack[c] - step_a * ws[par, c]
            wide = extend(par, c)
            for e in range(6):
                fresh = resid[c, e] - step_a * wide[e]
                resid[c, e] = fresh
                dirn[c, e] = fresh + step_b * dirn[c, e]
        for k, value in enumerate((norm_next, zeta_new, zeta, alpha, beta, gain, beta_shift)):
            state[k] = value

    one = jnp.ones((16, lanes), jnp.float32)
    none = jnp.zeros((16, lanes), jnp.float32)

    def body(step, carry):
        iterate(step, False)
        return carry

    for k, value in enumerate((norm, one, one, one, none, none, none)):
        state[k] = value
    lax.fori_loop(1, ITERS, body, 0)
    gain = iterate(ITERS, True)
    accumulate(gain)

    answer = [out_ref[c] for c in range(COMPS)]
    act[0, pl.ds(me_all, 1)] = dots([inner(spack, answer)])[None]
    total_devices = n_grp * n_all

    def send_act(p):
        copy(act.at[0, me_all], act.at[0, me_all], asend.at[p], arecv.at[me_all],
             place(lax.rem(me_all + p, total_devices))).start()

    def wait_act(p):
        there = lax.rem(me_all + total_devices - p, total_devices)
        done = copy(act.at[0, there], act.at[0, there], asend.at[p], arecv.at[there], place(there))
        done.wait_recv()
        done.wait_send()

    each(total_devices, send_act)
    each(total_devices, wait_act)
    sites = total_devices * cells_x * cells_t * lanes
    action_ref[...] = summed(act, 0, total_devices) * (1.0 / sites)


def on_device(sizes, source, links, shifts, residues, mass):
    n_grp, n_zt, n_xy = sizes
    cells_x, cells_t, lanes = source.shape[3:]
    n_all = n_zt * n_xy
    f32 = jnp.float32
    tiles = lambda *lead: pltpu.VMEM(lead + (8, lanes), f32)
    rows = lambda count: pltpu.VMEM((count, lanes), f32)
    nshift = shifts.shape[0]
    vmem = pl.BlockSpec(memory_space=pltpu.VMEM)
    smem = pl.BlockSpec(memory_space=pltpu.SMEM)
    dma = pltpu.SemaphoreType.DMA
    rational, action = pl.pallas_call(
        functools.partial(kernel, (n_grp, n_zt, n_xy, cells_x, cells_t)),
        out_shape=(
            jax.ShapeDtypeStruct((COMPS, 8, lanes), f32),
            jax.ShapeDtypeStruct((8, lanes), f32),
        ),
        in_specs=[vmem, vmem, smem, smem, smem],
        out_specs=(vmem, vmem),
        scratch_shapes=[
            tiles(4 * MAT), tiles(2, 4 * MAT), tiles(2, 2 * MAT), tiles(PAIRS), tiles(2, 2 * MAT), tiles(PAIRS),
            rows(40), rows(24), rows(24), rows(40), rows(24), rows(24),
            tiles(7, MAT, 4), tiles(COMPS, 6), tiles(COMPS, 6), tiles(COMPS, 6),
            tiles(nshift, COMPS), tiles(COMPS), tiles(2, COMPS), tiles(2, 4, COMPS),
            tiles(2, 4), tiles(2, 4), tiles(2, n_all), tiles(1, n_grp * n_all),
            pltpu.VMEM((7, 16, lanes), f32),
            dma((13,)), dma((13,)), dma((2, 8)), dma((2, 8)),
            dma((2, n_all)), dma((2, n_all)), dma((n_grp * n_all,)), dma((n_grp * n_all,)),
        ],
        compiler_params=pltpu.CompilerParams(collective_id=0, has_side_effects=True),
    )(
        source.reshape(COMPS, 8, lanes), links.reshape(2 * MAT, 8, lanes), shifts, residues, mass
    )
    return rational.reshape(source.shape), action[0, :1]


def solution(mesh):
    sizes = tuple(mesh.shape[name] for name in ("grp", "zt", "xy"))
    field = P("grp", None, None, "xy", "zt", None)
    return jax.shard_map(
        functools.partial(on_device, sizes),
        mesh=mesh,
        in_specs=(field, P("grp", None, None, None, "xy", "zt", None), P(), P(), P()),
        out_specs=(field, P()),
        check_vma=False,
    )
```

time: 513 us -> 77.1 us (0.15)
  blocking collectives: 293 us -> 0 us
  waiting for transfers between devices: 89.2 us -> 0 us
  Pallas kernels: 0 us -> 73 us
  starting transfers between devices: 64.4 us -> 0 us
  other arithmetic: 21.7 us -> 0 us
  between operations: 22 us -> 1.29 us
  local copies, waits for them, and re-layouts: 22.3 us -> 2.54 us
    psum x9 -> x0, blocking collectives: 285 us -> none  [the longest x7 214 us: on_device(): lax.psum((local_dot(direction, image), local_dot(residual, image), local_...]
    ppermute x66 -> x0, waiting for transfers between devices: 89.2 us -> none  [the longest x32 59.6 us: extended(): lax.ppermute(lax.slice_in_dim(block, block.shape[dim] - width, None, axis...]
    pallas_call x0 -> x1, Pallas kernels: none -> 73 us  [on_device(): pl.pallas_call(functools.partial(kernel, (n_grp, n_zt, n_xy, cells_x, cel...]
    ppermute x66 -> x0, starting transfers between devices: 64.4 us -> none  [the longest x32 41.5 us: extended(): lax.ppermute(lax.slice_in_dim(block, 0, width, axis=dim), axis, backward)]
    reduce_sum x74 -> x0, other arithmetic: 12.9 us -> none  [the longest x8 6.1 us: local_dot(): return jnp.sum(left * right, axis=(1, 2, 3, 4, 5))]
    another operation x227 -> x0, local copies, waits for them, and re-layouts: 12.4 us -> none  [the longest x118 6.2 us: times_link(): return jnp.stack([real, imag], axis=1)]
    all_gather x1 -> x0, blocking collectives: 7.77 us -> none  [on_device(): all_links = lax.all_gather(links, 'grp', axis=0, tiled=True)]
  transfers between devices with their start and end apart: 66 -> 0, of which waited for: 47 -> 0; matrix products, arithmetic and copies ran while one was open for 1% -> 0% of each run, Pallas kernels for 0% -> 0%
where the time goes in v1:
time: 77.1 us; the launch traced here: 76.9 us
  Pallas kernels  73 us (95%)
  local copies, waits for them, and re-layouts  2.54 us (3%)
  between operations  1.29 us (2%)
    pallas_call x1, Pallas kernels, on_device(): pl.pallas_call(functools.partial(kernel, (n_grp, n_zt, n_xy, cells_x, cel...  73 us

profile of v1, /device:TPU:0, one launch (start us, length us, event | category | flops | bytes accessed | tf_op | source)
XLA Modules:
  0.0 76.9 jit_solution(2561505388399316123)
XLA Ops:
  1.3 73.0 %shard_map.68 = (f32[6,8,128]{2,1,0:T(8,128)}, f32[8,128]{1,0:T(8,128)}) custom-call(f32[6,8,128]{2,1,0:T(8,128)} %bitcast.6, f32[36,8,128]{2,1,0:T(8,128)} %bitcast.4, f32[12]{0:T(128)} %shifts_ref.1, f32[12]{0:T(128)} %residues_ref.1, f32[1]{0:T(128)S(6)} %copy.8.mass_ref), custom_call_target="tpu_custom_call" | custom-call | tf_op jit(solution)/shard_map/pallas_call | solution.py:448
  74.3 1.2 %slice.3 = f32[1,1]{1,0:T(1,128)} slice(f32[8,128]{1,0:T(8,128)} %get-tuple-element.5), slice={[0:1], [0:1]} | slice | bytes 8 | tf_op jit(solution)/shard_map/slice | solution.py:470
  75.5 1.3 %copy.9 = f32[1,2,3,2,4,128]{5,4,3,2,1,0:T(4,128)} copy(f32[1,2,3,2,4,128]{5,4,3,2,1,0:T(4,128)} %bitcast.5) | data formatting | bytes 49152

commit v2 on v1

--- a/solution.py
+++ b/solution.py
@@ -73,6 +73,8 @@
     lane = lax.broadcasted_iota(jnp.int32, (8, lanes), 1)
     zcoord = lax.rem(lane, NZ)
     ycoord = lane // NZ
+    quarter = lanes // 4
+    home = sub == lane // quarter
     own = (sub >= 2) & (sub < 2 + cells_t)
     first = sub < cells_t
     late = lax.rem(sub, cells_t) >= 2
@@ -126,16 +128,21 @@
         tile = jnp.zeros((8, lanes), jnp.float32)
         for k, row in enumerate(rows):
             tile = jnp.where(sub == k, jnp.broadcast_to(jnp.sum(row, axis=0, keepdims=True), (8, lanes)), tile)
-        return tile
-
-    def summed(ref, par, count):
-        if count <= 32:
-            total = ref[par, 0]
-            for j in range(1, count):
-                total = total + ref[par, j]
+        tile = tile + roll(tile, 2 * quarter, 1)
+        tile = tile + roll(tile, quarter, 1)
+        return jnp.sum(jnp.where(home, tile, 0.0), axis=0, keepdims=True)
+
+    def summed(par):
+        if n_all <= 32:
+            level = [part[par, j] for j in range(n_all)]
+            while len(level) > 1:
+                odd = level[len(level) // 2 * 2:]
+                level = [level[k] + level[k + 1] for k in range(0, len(level) - 1, 2)] + odd
+            total = level[0]
         else:
-            total = lax.fori_loop(1, count, lambda j, acc: acc + ref[par, j], ref[par, 0])
-        return jnp.broadcast_to(jnp.sum(total, axis=1, keepdims=True), (8, lanes))
+            total = lax.fori_loop(1, n_all, lambda j, acc: acc + part[par, j], part[par, 0])
+        split = jnp.where(home, jnp.broadcast_to(total, (8, lanes)), 0.0)
+        return jnp.broadcast_to(jnp.sum(split, axis=1, keepdims=True), (8, lanes))
 
     def fill(values, k):
         return jnp.broadcast_to(values[k:k + 1], (16, lanes))
@@ -234,7 +241,7 @@
         for k in range(nshift):
             shiftdirs[k, c] = spack[c]
 
-    for item in near + far:
+    for item in near[2:] + far[2:4]:
         item.wait()
     to_pair.wait_send()
 
@@ -271,28 +278,35 @@
             return (0.5 * sign) * y_sign * value
         return sign * yz_sign * edge * value
 
-    for part_no in range(2):
-        for i in range(3):
-            for j in range(3):
-                c = part_no * PAIRS + i * 3 + j
-                flip = part_no * PAIRS + j * 3 + i
-                back = 1.0 if part_no else -1.0
-                for e in range(0, 5):
-                    wx = wide_link(0, c, e)
-                    if e > 0:
-                        gauge[0, c, e - 1] = wx
-                    if e < 4:
-                        gauge[1, flip, e] = back * wx
-                for e in range(1, 5):
-                    wz = wide_link(2, c, e)
-                    gauge[3, c, e - 1] = wz
-                    gauge[4, flip, e - 1] = back * z_dn(wz)
-                    wt = wide_link(3, c, e)
-                    gauge[5, c, e - 1] = wt
-                    gauge[6, flip, e - 1] = back * roll(wt, 1, 0)
-                    wy = wide_link(1, c, e)
-                    turned = wide_link(1, flip, e)
-                    gauge[2, c, e - 1] = wy + back * roll(turned, NZ, 1)
+    def build(rows):
+        for part_no in range(2):
+            for i in range(3):
+                for j in range(3):
+                    c = part_no * PAIRS + i * 3 + j
+                    flip = part_no * PAIRS + j * 3 + i
+                    back = 1.0 if part_no else -1.0
+                    for e in rows:
+                        wx = wide_link(0, c, e)
+                        if e > 0:
+                            gauge[0, c, e - 1] = wx
+                        if e < 4:
+                            gauge[1, flip, e] = back * wx
+                        if e == 0:
+                            continue
+                        wz = wide_link(2, c, e)
+                        gauge[3, c, e - 1] = wz
+                        gauge[4, flip, e - 1] = back * z_dn(wz)
+                        wt = wide_link(3, c, e)
+                        gauge[5, c, e - 1] = wt
+                        gauge[6, flip, e - 1] = back * roll(wt, 1, 0)
+                        wy = wide_link(1, c, e)
+                        turned = wide_link(1, flip, e)
+                        gauge[2, c, e - 1] = wy + back * roll(turned, NZ, 1)
+
+    build((2, 3))
+    for item in near[:2] + far[:2] + far[4:]:
+        item.wait()
+    build((0, 1, 4))
 
     def finish_halo(par):
         for item in halo(par):
@@ -305,7 +319,7 @@
         for e in range(6):
             dirn[c, e] = wide[e]
             resid[c, e] = wide[e]
-    norm = fill(summed(part, 0, n_all), 0)
+    norm = fill(summed(0), 0)
 
     def hop(field, e0):
         total = [None] * COMPS
@@ -363,11 +377,11 @@
                 shiftdirs[k, c] = zk * rpack[c] + bk * shiftdirs[k, c]
 
     def iterate(step, last):
-        norm, zeta, zeta_old, alpha_old, beta_old, gain, beta_shift = [state[k] for k in range(7)]
+        norm, zeta, zeta_old, alpha_old, beta_old, gain, beta_shift, along, score = [state[k] for k in range(9)]
         par = step % 2 if last else lax.rem(step, 2)
         packed, dpack = image_of()
         res = [rpack[c] for c in range(COMPS)]
-        part[par, pl.ds(me, 1)] = dots([inner(dpack, packed), inner(res, packed), inner(packed, packed)])[None]
+        part[par, pl.ds(me, 1)] = dots([inner(dpack, packed), inner(res, packed), inner(packed, packed), inner(spack, res)])[None]
         send_part(par)
         if not last:
             corner_tiles(packed, par)
@@ -377,15 +391,17 @@
                 item.start()
         catch_up(gain, zeta, beta_shift)
         wait_part(par)
-        sums = summed(part, par, n_all)
+        sums = summed(par)
         alpha = norm / fill(sums, 0)
         zeta_new = zeta * zeta_old * alpha_old / (
             alpha * beta_old * (zeta_old - zeta) + zeta_old * alpha_old * (1.0 + shift_rows * alpha)
         )
         ratio = zeta_new / zeta
+        along = zeta * fill(sums, 3) + beta_shift * along
         gain = residue_rows * alpha * ratio
+        score = score + gain * along
         if last:
-            return gain
+            return gain, score
         norm_next = norm - 2.0 * alpha * fill(sums, 1) + alpha * alpha * fill(sums, 2)
         beta = norm_next / norm
         beta_shift = beta * ratio * ratio
@@ -398,7 +414,7 @@
                 fresh = resid[c, e] - step_a * wide[e]
                 resid[c, e] = fresh
                 dirn[c, e] = fresh + step_b * dirn[c, e]
-        for k, value in enumerate((norm_next, zeta_new, zeta, alpha, beta, gain, beta_shift)):
+        for k, value in enumerate((norm_next, zeta_new, zeta, alpha, beta, gain, beta_shift, along, score)):
             state[k] = value
 
     one = jnp.ones((16, lanes), jnp.float32)
@@ -408,30 +424,31 @@
         iterate(step, False)
         return carry
 
-    for k, value in enumerate((norm, one, one, one, none, none, none)):
+    for k, value in enumerate((norm, one, one, one, none, none, none, none, none)):
         state[k] = value
     lax.fori_loop(1, ITERS, body, 0)
-    gain = iterate(ITERS, True)
+    gain, score = iterate(ITERS, True)
+    act[g] = jnp.sum(score, axis=0, keepdims=True)
+
+    def swap(p):
+        device = (lax.rem(g + p, n_grp), zt, xy)
+        return copy(act.at[g], act.at[g], asend.at[p], arecv.at[g], device)
+
+    def swapped(p):
+        there = lax.rem(g + n_grp - p, n_grp)
+        return copy(act.at[there], act.at[there], asend.at[p], arecv.at[there], (there, zt, xy))
+
+    for p in range(1, n_grp):
+        swap(p).start()
     accumulate(gain)
-
-    answer = [out_ref[c] for c in range(COMPS)]
-    act[0, pl.ds(me_all, 1)] = dots([inner(spack, answer)])[None]
-    total_devices = n_grp * n_all
-
-    def send_act(p):
-        copy(act.at[0, me_all], act.at[0, me_all], asend.at[p], arecv.at[me_all],
-             place(lax.rem(me_all + p, total_devices))).start()
-
-    def wait_act(p):
-        there = lax.rem(me_all + total_devices - p, total_devices)
-        done = copy(act.at[0, there], act.at[0, there], asend.at[p], arecv.at[there], place(there))
-        done.wait_recv()
-        done.wait_send()
-
-    each(total_devices, send_act)
-    each(total_devices, wait_act)
-    sites = total_devices * cells_x * cells_t * lanes
-    action_ref[...] = summed(act, 0, total_devices) * (1.0 / sites)
+    for p in range(1, n_grp):
+        swapped(p).wait_recv()
+        swap(p).wait_send()
+    total = act[0]
+    for k in range(1, n_grp):
+        total = total + act[k]
+    sites = n_grp * n_all * cells_x * cells_t * lanes
+    action_ref[0] = jnp.max(total) * (1.0 / sites)
 
 
 def on_device(sizes, source, links, shifts, residues, mass):
@@ -449,25 +466,25 @@
         functools.partial(kernel, (n_grp, n_zt, n_xy, cells_x, cells_t)),
         out_shape=(
             jax.ShapeDtypeStruct((COMPS, 8, lanes), f32),
-            jax.ShapeDtypeStruct((8, lanes), f32),
+            jax.ShapeDtypeStruct((1,), f32),
         ),
         in_specs=[vmem, vmem, smem, smem, smem],
-        out_specs=(vmem, vmem),
+        out_specs=(vmem, smem),
         scratch_shapes=[
             tiles(4 * MAT), tiles(2, 4 * MAT), tiles(2, 2 * MAT), tiles(PAIRS), tiles(2, 2 * MAT), tiles(PAIRS),
             rows(40), rows(24), rows(24), rows(40), rows(24), rows(24),
             tiles(7, MAT, 4), tiles(COMPS, 6), tiles(COMPS, 6), tiles(COMPS, 6),
             tiles(nshift, COMPS), tiles(COMPS), tiles(2, COMPS), tiles(2, 4, COMPS),
-            tiles(2, 4), tiles(2, 4), tiles(2, n_all), tiles(1, n_grp * n_all),
-            pltpu.VMEM((7, 16, lanes), f32),
+            tiles(2, 4), tiles(2, 4), pltpu.VMEM((2, n_all, 1, lanes), f32), pltpu.VMEM((n_grp, 1, lanes), f32),
+            pltpu.VMEM((9, 16, lanes), f32),
             dma((13,)), dma((13,)), dma((2, 8)), dma((2, 8)),
-            dma((2, n_all)), dma((2, n_all)), dma((n_grp * n_all,)), dma((n_grp * n_all,)),
+            dma((2, n_all)), dma((2, n_all)), dma((n_grp,)), dma((n_grp,)),
         ],
         compiler_params=pltpu.CompilerParams(collective_id=0, has_side_effects=True),
     )(
         source.reshape(COMPS, 8, lanes), links.reshape(2 * MAT, 8, lanes), shifts, residues, mass
     )
-    return rational.reshape(source.shape), action[0, :1]
+    return rational.reshape(source.shape), action
 
 
 def solution(mesh):

time: 77.1 us -> 68.1 us (0.88)
  Pallas kernels: 73 us -> 63.5 us
  between operations: 1.29 us -> 3.05 us
  local copies, waits for them, and re-layouts: 2.54 us -> 1.35 us
    pallas_call x1, Pallas kernels: 73 us -> 63.5 us  [on_device(): pl.pallas_call(functools.partial(kernel, (n_grp, n_zt, n_xy, cells_x, cel...]
    slice x1 -> x0, local copies, waits for them, and re-layouts: 1.19 us -> none  [on_device(): return (rational.reshape(source.shape), action[0, :1])]
where the time goes in v2:
time: 68.1 us; the launch traced here: 67.9 us
  Pallas kernels  63.5 us (93%)
  between operations  3.05 us (4%)
  local copies, waits for them, and re-layouts  1.35 us (2%)
    pallas_call x1, Pallas kernels, on_device(): pl.pallas_call(functools.partial(kernel, (n_grp, n_zt, n_xy, cells_x, cel...  63.5 us

profile of v2, /device:TPU:0, one launch (start us, length us, event | category | flops | bytes accessed | tf_op | source)
XLA Modules:
  0.0 67.9 jit_solution(9178399103424106143)
XLA Ops:
  1.3 63.5 %shard_map.68 = (f32[6,8,128]{2,1,0:T(8,128)}, f32[1]{0:T(128)}) custom-call(f32[6,8,128]{2,1,0:T(8,128)} %bitcast.5, f32[36,8,128]{2,1,0:T(8,128)} %bitcast.3, f32[12]{0:T(128)} %shifts_ref.1, f32[12]{0:T(128)} %residues_ref.1, f32[1]{0:T(128)S(6)} %copy.9.mass_ref), custom_call_target="tpu_custom_call" | custom-call | tf_op jit(solution)/shard_map/pallas_call | solution.py:465
  64.8 1.3 %copy.10 = f32[1,2,3,2,4,128]{5,4,3,2,1,0:T(4,128)} copy(f32[1,2,3,2,4,128]{5,4,3,2,1,0:T(4,128)} %bitcast.4) | data formatting | bytes 49152

commit v3 on v2

--- a/solution.py
+++ b/solution.py
@@ -21,10 +21,10 @@
 
 
 def kernel(
-    dims, source_ref, links_ref, shifts_ref, residues_ref, mass_ref, out_ref, action_ref,
+    dims, source_hbm, links_hbm, shifts_ref, residues_ref, mass_ref, out_ref, action_ref,
     lk, tfar, xfar, xtwo, sx, sx2, cs_ll, cs_hl, cs_lh, c_ll, c_hl, c_lh,
     gauge, dirn, resid, mid, shiftdirs, rpack, ws, wr, cs, cr, part, act,
-    state, lsend, lrecv, hsend, hrecv, psend, precv, asend, arecv,
+    state, source_ref, links_ref, isem, lsend, lrecv, hsend, hrecv, psend, precv, asend, arecv,
 ):
     n_grp, n_zt, n_xy, cells_x, cells_t = dims
     lanes = NY * NZ
@@ -67,7 +67,13 @@
             device_id_type=pl.DeviceIdType.MESH,
         )
 
+    fetch_links = pltpu.make_async_copy(links_hbm, links_ref, isem.at[0])
+    fetch_source = pltpu.make_async_copy(source_hbm, source_ref, isem.at[1])
+    fetch_links.start()
+    fetch_source.start()
     each(n_grp * n_all, greet)
+    fetch_links.wait()
+    fetch_source.wait()
 
     sub = lax.broadcasted_iota(jnp.int32, (8, lanes), 0)
     lane = lax.broadcasted_iota(jnp.int32, (8, lanes), 1)
@@ -468,7 +474,7 @@
             jax.ShapeDtypeStruct((COMPS, 8, lanes), f32),
             jax.ShapeDtypeStruct((1,), f32),
         ),
-        in_specs=[vmem, vmem, smem, smem, smem],
+        in_specs=[pl.BlockSpec(memory_space=pl.ANY)] * 2 + [smem] * 3,
         out_specs=(vmem, smem),
         scratch_shapes=[
             tiles(4 * MAT), tiles(2, 4 * MAT), tiles(2, 2 * MAT), tiles(PAIRS), tiles(2, 2 * MAT), tiles(PAIRS),
@@ -476,7 +482,7 @@
             tiles(7, MAT, 4), tiles(COMPS, 6), tiles(COMPS, 6), tiles(COMPS, 6),
             tiles(nshift, COMPS), tiles(COMPS), tiles(2, COMPS), tiles(2, 4, COMPS),
             tiles(2, 4), tiles(2, 4), pltpu.VMEM((2, n_all, 1, lanes), f32), pltpu.VMEM((n_grp, 1, lanes), f32),
-            pltpu.VMEM((9, 16, lanes), f32),
+            pltpu.VMEM((9, 16, lanes), f32), tiles(COMPS), tiles(2 * MAT), dma((2,)),
             dma((13,)), dma((13,)), dma((2, 8)), dma((2, 8)),
             dma((2, n_all)), dma((2, n_all)), dma((n_grp,)), dma((n_grp,)),
         ],

time: 68.1 us -> 67.9 us (level)
  no operation moved by 1% of the time
where the time goes in v3:
time: 67.9 us; the launch traced here: 67.7 us
  Pallas kernels  63.3 us (93%)
  between operations  3.05 us (4%)
  local copies, waits for them, and re-layouts  1.35 us (2%)
    pallas_call x1, Pallas kernels, on_device(): pl.pallas_call(functools.partial(kernel, (n_grp, n_zt, n_xy, cells_x, cel...  63.3 us

profile of v3, /device:TPU:0, one launch (start us, length us, event | category | flops | bytes accessed | tf_op | source)
XLA Modules:
  0.0 67.7 jit_solution(3910357228975687501)
XLA Ops:
  1.3 63.3 %shard_map.68 = (f32[6,8,128]{2,1,0:T(8,128)}, f32[1]{0:T(128)}) custom-call(f32[6,8,128]{2,1,0:T(8,128)} %bitcast.5, f32[36,8,128]{2,1,0:T(8,128)} %bitcast.3, f32[12]{0:T(128)} %shifts_ref.1, f32[12]{0:T(128)} %residues_ref.1, f32[1]{0:T(128)S(6)} %copy.9.mass_ref), custom_call_target="tpu_custom_call" | custom-call | tf_op jit(solution)/shard_map/pallas_call | solution.py:471
  64.5 1.3 %copy.10 = f32[1,2,3,2,4,128]{5,4,3,2,1,0:T(4,128)} copy(f32[1,2,3,2,4,128]{5,4,3,2,1,0:T(4,128)} %bitcast.4) | data formatting | bytes 49152
